TPU v7x, 32 devices: a whole 2x2x4 slice. The times are simulated.
32 devices in a mesh: fsdp: 4 (over y, x), context: 2 (over core), tensor: 4 (over z).
Axes of the slice: x: 2, y: 2, z: 4, core: 2. Of those that a mesh axis runs over, the one named last changes fastest.
Arguments:
- tokens: bfloat16 [1024, 4, 1024], P('context', 'fsdp'), may hold values from -6 to 6
- out_grad: bfloat16 [1024, 4, 1024], P('context', 'fsdp'), may hold values from -6 to 6
- weight_stack: bfloat16 [4, 4, 1312, 1024], P('fsdp', 'tensor', 'context'), as said below
- muon_state: float32 [4, 4, 1312, 1024], P('fsdp', 'tensor', 'context'), as said below
- norm_gains: float32 [2, 1024], replicated, may hold values from 0.5 to 1.5
- adam_first: float32 [2, 1024], replicated, may hold values from -112 to 112
- adam_second: float32 [2, 1024], replicated, may hold values from 122.88 to 1228.8
- segment_ids: int32 [1024, 4], P(None, 'fsdp'), may hold values from 0 to 1024, as said below
- position_ids: int32 [1024, 4], P('context', 'fsdp'), may hold values from 0 to 1023, as said below
Outputs:
- layer_out: bfloat16 [1024, 4, 1024], P('context', 'fsdp')
- tokens_grad: bfloat16 [1024, 4, 1024], P('context', 'fsdp')
- weight_grads: float32 [4, 4, 1312, 1024], P('fsdp', 'tensor', 'context')
- muon_next: float32 [4, 4, 1312, 1024], P('fsdp', 'tensor', 'context')
- weight_update: float32 [4, 4, 1312, 1024], P('fsdp', 'tensor', 'context')
- direction_scale: float32 [4], P('fsdp')
- gain_grads: float32 [2, 1024], replicated
- adam_first_next: float32 [2, 1024], replicated
- adam_second_next: float32 [2, 1024], replicated
- gain_update: float32 [2, 1024], replicated
Inputs may be any that keep to these rules, and one draw needn't show every extreme that they name: `segment_ids`: along a sequence the nonzero ids start at 1 and rise by at most one from one token to the next; id 0 marks padding, a possibly empty run of tokens at the end of a sequence. `position_ids`: A token's offset from the first token of its document, or of the padding run. `weight_stack`: rows of a block beyond its weight's row count (R_k of the steps) are zero. `muon_state`: rows of a block beyond its weight's row count are zero.
All inputs are finite; a program needn't handle non-finite values.
Results may differ from a plain program's by a relative error of at most 0.035.
Values may be sent and summed in bfloat16 or wider, within the bound.
A program may use at most 192 MiB of HBM per device.

v0:
```python
import math

import jax
import jax.numpy as jnp
from jax import lax
from jax.experimental import pallas as pl
from jax.experimental.pallas import tpu as pltpu
from jax.sharding import PartitionSpec as P

D = 1024
HEADS = 16
HEAD_DIM = 64
FF = 2624
ITERS = 5
STEP = 8


rope_base = 160000.0
norm_eps = 1e-05
ns_first = 3.4445
ns_second = -4.775
ns_third = 2.0315
muon_beta = 0.5
muon_rate = 0.15
decay_rate = 0.1
adam_beta = 0.5
adam_rate = 0.05
ortho_eps = 1e-07
adam_eps = 1e-08
precision_highest = lax.Precision.HIGHEST


def layer_norm(values, gain_row):
    centre = values - jnp.mean(values, axis=-1, keepdims=True)
    spread = jnp.mean(centre * centre, axis=-1, keepdims=True)
    return centre * lax.rsqrt(spread + norm_eps) * gain_row


def rope_tables(positions, head_width):
    half_width = head_width // 2
    freqs = rope_base ** (-(jnp.arange(half_width, dtype=jnp.float32) * 2.0 / head_width))
    angle = positions.astype(jnp.float32)[..., None] * freqs
    angle = jnp.concatenate([angle, angle], axis=-1)
    return (jnp.cos(angle), jnp.sin(angle))


def rotate(values, cosine, sine_table):
    half_width = values.shape[-1] // 2
    turned = jnp.concatenate([-values[..., half_width:], values[..., :half_width]], axis=-1)
    return values * cosine + turned * sine_table


def rotate_back(grads_in, cosine, sine_table):
    half_width = grads_in.shape[-1] // 2
    scaled = grads_in * sine_table
    turned = jnp.concatenate([scaled[..., half_width:], -scaled[..., :half_width]], axis=-1)
    return grads_in * cosine + turned


def project(left_rows, right_rows):
    return lax.dot_general(
        left_rows, right_rows, (((1,), (1,)), ((), ())), preferred_element_type=jnp.float32
    )


def contract_exact(left_rows, right_rows):
    return lax.dot_general(
        left_rows,
        right_rows,
        (((0,), (0,)), ((), ())),
        precision=precision_highest,
        preferred_element_type=jnp.float32,
    )


def geglu_gate(gate_part, up_part):
    return jax.nn.gelu(gate_part, approximate=False) * up_part


def per_device(
    tokens,
    out_grad,
    weight_stack,
    muon_state,
    norm_gains,
    adam_first,
    adam_second,
    segment_ids,
    position_ids,
):
    local_len, seq_count, model_width = tokens.shape
    token_count = local_len * seq_count
    groups = lax.axis_size("tensor")
    contexts = lax.axis_size("context")
    full_len = local_len * contexts
    local_rows = weight_stack.shape[2]
    pad_rows = local_rows * contexts
    heads_dev = HEADS // groups
    ff_dev = FF // groups
    inner_width = heads_dev * HEAD_DIM
    counts = (3 * inner_width, inner_width, 2 * ff_dev, ff_dev)
    score_scale = HEAD_DIM ** (-0.5)
    own_block = weight_stack.reshape(local_rows, model_width)
    gathered = lax.all_gather(own_block, ("fsdp", "context"), axis=0, tiled=True).reshape(
        4, pad_rows, model_width
    )
    w_qkv = gathered[0, : counts[0]]
    w_out = gathered[1, : counts[1]]
    w_in = gathered[2, : counts[2]]
    w_down = gathered[3, : counts[3]]
    inputs = tokens.astype(jnp.float32).reshape(token_count, model_width)
    act_in = layer_norm(inputs, norm_gains[0]).astype(jnp.bfloat16)
    projected = project(act_in, w_qkv).reshape(local_len, seq_count, 3, heads_dev, HEAD_DIM)
    cosine, sine_table = rope_tables(position_ids, HEAD_DIM)
    rot_cos = cosine[:, :, None, :]
    rot_sin = sine_table[:, :, None, :]
    query_matrix = rotate(projected[:, :, 0], rot_cos, rot_sin).astype(jnp.bfloat16)
    key_matrix_rows = rotate(projected[:, :, 1], rot_cos, rot_sin).astype(jnp.bfloat16)
    value_matrix_rows = projected[:, :, 2].astype(jnp.bfloat16)
    key_value = jnp.concatenate(
        [
            key_matrix_rows.reshape(local_len, seq_count, inner_width),
            value_matrix_rows.reshape(local_len, seq_count, inner_width),
        ],
        axis=-1,
    )
    key_value_all = lax.all_gather(key_value, "context", axis=0, tiled=True)
    keys_all = key_value_all[..., :inner_width].reshape(full_len, seq_count, heads_dev, HEAD_DIM)
    values_all = key_value_all[..., inner_width:].reshape(full_len, seq_count, heads_dev, HEAD_DIM)
    offset = lax.axis_index("context") * local_len
    seg_query = lax.dynamic_slice_in_dim(segment_ids, offset, local_len, 0)
    same_doc = seg_query.T[:, :, None] == segment_ids.T[:, None, :]
    keep_mask = (seg_query > 0).astype(jnp.float32)
    unscaled_score = jnp.einsum(
        "lshd,mshd->shlm", query_matrix, keys_all, preferred_element_type=jnp.float32
    )
    scores = jnp.where(same_doc[:, None], unscaled_score * score_scale, -jnp.inf)
    row_max = jnp.max(scores, axis=-1, keepdims=True)
    log_total = row_max + jnp.log(jnp.sum(jnp.exp(scores - row_max), axis=-1, keepdims=True))
    probs_low = jnp.exp(scores - log_total).astype(jnp.bfloat16)
    attended = jnp.einsum(
        "shlm,mshd->lshd", probs_low, values_all, preferred_element_type=jnp.float32
    )
    attn_in = (
        (attended * keep_mask[:, :, None, None])
        .astype(jnp.bfloat16)
        .reshape(token_count, inner_width)
    )
    branch_one = lax.psum(
        jnp.dot(attn_in, w_out, preferred_element_type=jnp.float32).astype(jnp.bfloat16), "tensor"
    ).astype(jnp.float32)
    resid = inputs + branch_one
    mlp_in = layer_norm(resid, norm_gains[1]).astype(jnp.bfloat16)
    mixed_rows = project(mlp_in, w_in)
    hidden_full, geglu_pull = jax.vjp(geglu_gate, mixed_rows[:, :ff_dev], mixed_rows[:, ff_dev:])
    hidden = hidden_full.astype(jnp.bfloat16)
    branch_two = lax.psum(
        jnp.dot(hidden, w_down, preferred_element_type=jnp.float32).astype(jnp.bfloat16), "tensor"
    ).astype(jnp.float32)
    layer_out = (resid + branch_two).astype(jnp.bfloat16).reshape(local_len, seq_count, model_width)
    out_cot = out_grad.astype(jnp.float32).reshape(token_count, model_width)
    dbranch_two = out_cot.astype(jnp.bfloat16)
    dhidden = project(dbranch_two, w_down)
    dgate, dup_part = geglu_pull(dhidden)
    dmixed = jnp.concatenate([dgate, dup_part], axis=1).astype(jnp.bfloat16)
    dnormed_two = lax.psum(
        jnp.dot(dmixed, w_in, preferred_element_type=jnp.float32).astype(jnp.bfloat16), "tensor"
    ).astype(jnp.float32)
    norm_two_out, norm_two_pull = jax.vjp(layer_norm, resid, norm_gains[1])
    dresid_norm, dgain_two = norm_two_pull(dnormed_two)
    dresid = out_cot + dresid_norm
    dbranch_one = dresid.astype(jnp.bfloat16)
    keep_low = keep_mask.reshape(token_count, 1).astype(jnp.bfloat16)
    dattended = project(dbranch_one, w_out).astype(jnp.bfloat16) * keep_low
    dattn = dattended.reshape(local_len, seq_count, heads_dev, HEAD_DIM)
    dquery_list = []
    dkey_list = []
    dvalue_list = []
    for head_index in range(heads_dev):
        query_head = query_matrix[:, :, head_index]
        key_head = keys_all[:, :, head_index]
        value_head = values_all[:, :, head_index]
        dout_head = dattn[:, :, head_index]
        raw_head = jnp.einsum(
            "lsd,msd->slm", query_head, key_head, preferred_element_type=jnp.float32
        )
        prob_head = jnp.exp(
            jnp.where(same_doc, raw_head * score_scale, -jnp.inf) - log_total[:, head_index]
        )
        dprob = jnp.einsum(
            "lsd,msd->slm", dout_head, value_head, preferred_element_type=jnp.float32
        )
        delta = jnp.sum(prob_head * dprob, axis=-1, keepdims=True)
        dscore = (prob_head * (dprob - delta) * score_scale).astype(jnp.bfloat16)
        dquery_list.append(
            jnp.einsum("slm,msd->lsd", dscore, key_head, preferred_element_type=jnp.float32)
        )
        dkey_head = jnp.einsum(
            "slm,lsd->msd", dscore, query_head, preferred_element_type=jnp.float32
        )
        dvalue_head = jnp.einsum(
            "slm,lsd->msd",
            prob_head.astype(jnp.bfloat16),
            dout_head,
            preferred_element_type=jnp.float32,
        )
        summed = lax.psum_scatter(
            jnp.concatenate([dkey_head, dvalue_head], axis=-1).astype(jnp.bfloat16),
            "context",
            scatter_dimension=0,
            tiled=True,
        ).astype(jnp.float32)
        dkey_list.append(summed[..., :HEAD_DIM])
        dvalue_list.append(summed[..., HEAD_DIM:])
    dqueries = jnp.stack(dquery_list, axis=2)
    dkeys = jnp.stack(dkey_list, axis=2)
    dvalues = jnp.stack(dvalue_list, axis=2)
    dprojected = (
        jnp.stack(
            [
                rotate_back(dqueries, rot_cos, rot_sin),
                rotate_back(dkeys, rot_cos, rot_sin),
                dvalues,
            ],
            axis=2,
        )
        .astype(jnp.bfloat16)
        .reshape(token_count, 3 * inner_width)
    )
    dnormed_one = lax.psum(
        jnp.dot(dprojected, w_qkv, preferred_element_type=jnp.float32).astype(jnp.bfloat16),
        "tensor",
    ).astype(jnp.float32)
    norm_one_out, norm_one_pull = jax.vjp(layer_norm, inputs, norm_gains[0])
    dinput_norm, dgain_one = norm_one_pull(dnormed_one)
    tokens_grad = (
        (dresid + dinput_norm).astype(jnp.bfloat16).reshape(local_len, seq_count, model_width)
    )
    gain_grads = lax.psum(jnp.stack([dgain_one, dgain_two]), ("fsdp", "context"))

    def padded(block, used_rows):
        return jnp.pad(block, ((0, 0), (0, pad_rows - used_rows)))

    left_rows = jnp.concatenate(
        [
            padded(dprojected, counts[0]),
            padded(attn_in, counts[1]),
            padded(dmixed, counts[2]),
            padded(hidden, counts[3]),
        ],
        axis=1,
    )
    right_rows = jnp.stack([act_in, dbranch_one, mlp_in, dbranch_two])
    blocks = local_rows * lax.axis_size(("fsdp", "context")) // pad_rows
    col_block = left_rows.reshape(token_count, blocks, pad_rows)
    grad_block = lax.psum_scatter(
        jnp.einsum(
            "nbp,bnd->bpd", col_block, right_rows, preferred_element_type=jnp.float32
        ).reshape(local_rows * lax.axis_size(("fsdp", "context")), model_width),
        ("fsdp", "context"),
        scatter_dimension=0,
        tiled=True,
    )
    momentum = muon_state.reshape(local_rows, model_width)
    muon_next = muon_beta * momentum + (1.0 - muon_beta) * grad_block
    direction = (1.0 - muon_beta) * grad_block + muon_beta * muon_next
    norm_total = lax.psum(jnp.sum(direction * direction), ("context", "tensor"))
    norm_size = jnp.sqrt(norm_total)
    direction_scale = jnp.log(norm_size).reshape(1)
    ortho_local = direction / (norm_size + ortho_eps)
    ortho_block = lax.all_gather(
        ortho_local.astype(jnp.bfloat16), "context", axis=0, tiled=True
    ).astype(ortho_local.dtype)
    for sweep_index in range(ITERS):
        gram_sum = lax.psum(
            contract_exact(ortho_block, ortho_block).astype(jnp.bfloat16), "tensor"
        ).astype(jnp.float32)
        square = jnp.dot(
            gram_sum, gram_sum, precision=precision_highest, preferred_element_type=jnp.float32
        )
        mix_matrix = ns_second * gram_sum + ns_third * square
        ortho_block = ns_first * ortho_block + jnp.dot(
            ortho_block, mix_matrix, precision=precision_highest, preferred_element_type=jnp.float32
        )
    own_rows = lax.dynamic_slice_in_dim(
        ortho_block, lax.axis_index("context") * local_rows, local_rows, 0
    )
    owner_index = lax.axis_index("fsdp")
    spreads = jnp.array(
        [0.2 * math.sqrt(3 * D), 0.2 * math.sqrt(D), 0.2 * math.sqrt(2 * FF), 0.2 * math.sqrt(FF)],
        jnp.float32,
    )
    spread = jnp.sum(jnp.where(jnp.arange(4) == owner_index, spreads, 0.0))
    old_weight = own_block.astype(jnp.float32)
    weight_update = -muon_rate * (spread * own_rows + decay_rate * old_weight)
    adam_first_next = adam_beta * adam_first + (1.0 - adam_beta) * gain_grads
    adam_second_next = adam_beta * adam_second + (1.0 - adam_beta) * gain_grads * gain_grads
    correction = 1.0 - adam_beta**STEP
    gain_update = -adam_rate * (
        adam_first_next / correction / (jnp.sqrt(adam_second_next / correction) + adam_eps)
        + decay_rate * norm_gains
    )
    block_shape = (1, 1, local_rows, model_width)
    return (
        layer_out,
        tokens_grad,
        grad_block.reshape(block_shape),
        muon_next.reshape(block_shape),
        weight_update.reshape(block_shape),
        direction_scale,
        gain_grads,
        adam_first_next,
        adam_second_next,
        gain_update,
    )


MESH_ID = pl.DeviceIdType.MESH
ANY = pl.ANY


def ring_place(index):
    return index + index // 2 - 2 * (index // 3)


def split_units(rows, parts, unit=16):
    units = rows // unit
    sizes = [(units // parts + (1 if i < units % parts else 0)) * unit for i in range(parts)]
    return [s for s in sizes if s]


def ring_chunks(counts, local_rows, which, core, target):
    first = core * local_rows
    rows = min(counts[which], first + local_rows) - first
    if rows <= 0:
        return [[], []]
    halves = split_units(rows, 2)
    if len(halves) == 1:
        halves = halves + [0]
    out, at = [], first
    for half in halves:
        pieces = []
        if half:
            for size in split_units(half, max(1, round(half / target))):
                pieces.append((at, size))
                at += size
        out.append(pieces)
    return out


class Place:
    def __init__(self):
        self.f = lax.axis_index("fsdp")
        self.c = lax.axis_index("context")
        self.t = lax.axis_index("tensor")
        self.pos = ring_place(self.f)
        self.next = ring_place((self.pos + 1) % 4)
        self.prev = ring_place((self.pos + 3) % 4)
        homes = (0, 1, 3, 2)
        self.hops = [[(self.pos + 4 - home) % 4, (home + 4 - self.pos) % 4] for home in homes]
        self.outer = jnp.logical_or(self.t == 0, self.t == 3)
        self.inner_mate = jnp.where(self.t == 0, 1, 2)
        self.outer_mate = jnp.where(self.t == 1, 0, 3)

    def ring(self, direction):
        return (self.next if direction == 0 else self.prev, self.c, self.t)

    def partner(self):
        return (self.f, 1 - self.c, self.t)

    def chip_z(self, z):
        return (self.f, self.c, z)

    def hop(self, which, direction):
        return self.hops[which][direction]


def greet(place, ring, partner, line):
    barrier = pltpu.get_barrier_semaphore()

    def signal(device):
        pl.semaphore_signal(barrier, inc=1, device_id=device, device_id_type=MESH_ID)

    count = 0
    if ring:
        signal(place.ring(0))
        signal(place.ring(1))
        count += 2
    if partner:
        signal(place.partner())
        count += 1
    if line:
        @pl.when(place.outer)
        def _():
            signal(place.chip_z(place.inner_mate))
            pl.semaphore_wait(barrier, count + 1)

        @pl.when(jnp.logical_not(place.outer))
        def _():
            signal(place.chip_z(place.outer_mate))
            signal(place.chip_z(3 - place.t))
            pl.semaphore_wait(barrier, count + 2)
    else:
        pl.semaphore_wait(barrier, count)


def remote(src, dst, send, recv, device):
    return pltpu.make_async_remote_copy(
        src_ref=src, dst_ref=dst, send_sem=send, recv_sem=recv, device_id=device, device_id_type=MESH_ID
    )


def run_steps(*tracks):
    total = max(len(track) for track in tracks)
    done = [0] * len(tracks)
    for index in range(total):
        for number, track in enumerate(tracks):
            upto = -(-len(track) * (index + 1) // total)
            while done[number] < upto:
                track[done[number]]()
                done[number] += 1


def gather_plan(counts, local_rows, ks, target=96):
    plan = []
    for core in (0, 1):
        ident = 0
        for which in ks:
            for direction, pieces in enumerate(ring_chunks(counts, local_rows, which, core, target)):
                for order, (row, rows) in enumerate(pieces):
                    plan.append((ident, which, core, direction, order, row, rows))
                    ident += 1
    return plan, max(p[0] for p in plan) + 1


def gather_steps(place, plan, local_rows, base, own_ref, out_ref, sems, skew=2):
    ss, rs, sp, rp = sems

    def dst(which, row, rows):
        return out_ref.at[pl.ds(base[which] + row, rows)]

    def src(core, row, rows):
        return own_ref.at[pl.ds(row - core * local_rows, rows)]

    def begin():
        for ident, which, core, direction, order, row, rows in plan:
            @pl.when(jnp.logical_and(place.c == core, place.f == which))
            def _():
                remote(src(core, row, rows), dst(which, row, rows), ss.at[ident], rs.at[ident],
                       place.ring(direction)).start()
        for ident, which, core, direction, order, row, rows in plan:
            @pl.when(jnp.logical_and(place.c == core, place.f == which))
            def _():
                remote(src(core, row, rows), dst(which, row, rows), sp.at[ident], rp.at[ident],
                       place.partner()).start()

    ordered = sorted(plan, key=lambda p: (p[4], p[1]))
    last = max(p[4] for p in plan)

    def visit(item, role):
        ident, which, core, direction, order, row, rows = item
        mine = dst(which, row, rows)

        @pl.when(jnp.logical_and(place.c == core, place.hop(which, direction) == role))
        def _():
            remote(mine, mine, ss.at[ident], rs.at[ident], place.ring(direction)).wait_recv()
            if role <= 2:
                remote(mine, mine, ss.at[ident], rs.at[ident], place.ring(direction)).start()
            remote(mine, mine, sp.at[ident], rp.at[ident], place.partner()).start()

    def step(j):
        def run():
            for role in (1, 2, 3):
                for item in ordered:
                    if item[4] == j - skew * (role - 1):
                        visit(item, role)
        return run

    def ready():
        for ident, which, core, direction, order, row, rows in plan:
            mine = dst(which, row, rows)

            @pl.when(place.c == 1 - core)
            def _():
                remote(mine, mine, sp.at[ident], rp.at[ident], place.partner()).wait_recv()

    def end():
        for ident, which, core, direction, order, row, rows in plan:
            hop = place.hop(which, direction)
            mine = dst(which, row, rows)

            @pl.when(jnp.logical_and(place.c == core, hop <= 2))
            def _():
                remote(mine, mine, ss.at[ident], rs.at[ident], place.ring(direction)).wait_send()

            @pl.when(place.c == core)
            def _():
                remote(mine, mine, sp.at[ident], rp.at[ident], place.partner()).wait_send()

    return begin, [step(j) for j in range(last + 1 + 2 * skew)], ready, end


def line_steps(place, chunks, own, out, early, mid, low, sems, lag=2, back_lag=3, prep=None, done=None):
    s1, r1, s2, r2, s3, r3 = sems

    def from_end(i, device):
        return remote(own(i), early(i), s1.at[i], r1.at[i], device)

    def across(i):
        return remote(mid(i), low(i), s2.at[i], r2.at[i], place.chip_z(3 - place.t))

    def back(i, device):
        return remote(out(i), out(i), s3.at[i], r3.at[i], device)

    def step(i):
        def run():
            if i < chunks and prep is not None:
                prep(i)

            @pl.when(place.outer)
            def _():
                if i < chunks:
                    from_end(i, place.chip_z(place.inner_mate)).start()
                if 0 <= i - lag - back_lag < chunks:
                    back(i - lag - back_lag, place.chip_z(place.inner_mate)).wait_recv()

            @pl.when(jnp.logical_not(place.outer))
            def _():
                if i < chunks:
                    from_end(i, place.chip_z(place.outer_mate)).wait_recv()
                    pair = own(i)[...].astype(jnp.float32) + early(i)[...].astype(jnp.float32)
                    mid(i)[...] = pair.astype(mid(i).dtype)
                    across(i).start()
                j = i - lag
                if 0 <= j < chunks:
                    across(j).wait_recv()
                    total = mid(j)[...].astype(jnp.float32) + low(j)[...].astype(jnp.float32)
                    out(j)[...] = total.astype(out(j).dtype)
                    back(j, place.chip_z(place.outer_mate)).start()
            if done is not None:
                if 0 <= i - lag - back_lag < chunks:
                    done(i - lag - back_lag)
        return run

    def end():
        @pl.when(place.outer)
        def _():
            for i in range(chunks):
                from_end(i, place.chip_z(place.inner_mate)).wait_send()

        @pl.when(jnp.logical_not(place.outer))
        def _():
            for i in range(chunks):
                across(i).wait_send()
                back(i, place.chip_z(place.outer_mate)).wait_send()

    return [step(i) for i in range(chunks + lag + back_lag)], end


def scatter_steps(place, plan, local_rows, base, part_ref, grad_ref, prx, rrx, tx, sems, skew=2):
    ss, rs, sp, rp = sems

    def rows_of(ref, which, row, rows):
        return ref.at[pl.ds(base[which] + row, rows)]

    def partner_copy(item):
        ident, which, core, direction, order, row, rows = item
        return remote(rows_of(part_ref, which, row, rows), rows_of(prx, which, row, rows),
                      sp.at[ident], rp.at[ident], place.partner())

    def ring_copy(item):
        ident, which, core, direction, order, row, rows = item
        return remote(rows_of(tx, which, row, rows), rows_of(rrx, which, row, rows),
                      ss.at[ident], rs.at[ident], place.ring(direction))

    ordered = sorted(plan, key=lambda p: (p[4], p[1]))
    last = max(p[4] for p in plan)

    def begin(ks):
        for item in ordered:
            if item[1] in ks:
                @pl.when(place.c == 1 - item[2])
                def _():
                    partner_copy(item).start()

    def visit(item, late):
        ident, which, core, direction, order, row, rows = item
        hop = place.hop(which, direction)
        role = (late + 1) % 4

        @pl.when(jnp.logical_and(place.c == core, hop == role))
        def _():
            partner_copy(item).wait_recv()
            total = (rows_of(part_ref, which, row, rows)[...].astype(jnp.float32)
                     + rows_of(prx, which, row, rows)[...].astype(jnp.float32))
            if role != 1:
                ring_copy(item).wait_recv()
                total = total + rows_of(rrx, which, row, rows)[...].astype(jnp.float32)
            if role == 0:
                grad_ref[pl.ds(row - core * local_rows, rows)] = total
            else:
                rows_of(tx, which, row, rows)[...] = total.astype(tx.dtype)
                ring_copy(item).start()

    def step(j):
        def run():
            for late in range(4):
                for item in ordered:
                    if item[4] == j - skew * late:
                        visit(item, late)
        return run

    def end():
        for item in plan:
            ident, which, core, direction, order, row, rows = item

            @pl.when(place.c == 1 - core)
            def _():
                partner_copy(item).wait_send()

            @pl.when(jnp.logical_and(place.c == core, place.hop(which, direction) != 0))
            def _():
                ring_copy(item).wait_send()

    return begin, [step(j) for j in range(last + 1 + 3 * skew)], end


VMEM_SPEC = pl.BlockSpec(memory_space=pltpu.VMEM)
ANY_SPEC = pl.BlockSpec(memory_space=pl.ANY)


def dma(count):
    return pltpu.SemaphoreType.DMA((count,))


def comm_call(kernel, outs, ins, in_specs, out_specs, scratch, ident):
    return pl.pallas_call(
        kernel,
        out_shape=outs,
        in_specs=in_specs,
        out_specs=out_specs,
        scratch_shapes=scratch,
        compiler_params=pltpu.CompilerParams(
            collective_id=ident, has_side_effects=True, vmem_limit_bytes=60 * 2**20
        ),
    )(*ins)


def base_rows(counts, ks):
    base, at = {}, 0
    for which in ks:
        base[which] = at
        at += counts[which]
    return base, at


def own_rows_copy(place, counts, local_rows, ks, base, own_ref, out_ref, sem, act):
    for which in ks:
        for core in (0, 1):
            rows = min(counts[which] - core * local_rows, local_rows)
            if rows > 0:
                @pl.when(jnp.logical_and(place.c == core, place.f == which))
                def _():
                    act(pltpu.make_async_copy(
                        own_ref.at[pl.ds(0, rows)],
                        out_ref.at[pl.ds(base[which] + core * local_rows, rows)],
                        sem.at[0],
                    ))


class LineSum:
    def __init__(self, place, rows, own, early, mid, low, total, sems):
        self.place, self.rows = place, rows
        self.own, self.early, self.mid, self.low, self.total = own, early, mid, low, total
        self.sems = sems

    def cut(self, ref, i):
        return ref.at[pl.ds(pl.multiple_of(i * self.rows, self.rows), self.rows)]

    def from_end(self, i, mate):
        s1, r1 = self.sems[:2]
        return remote(self.cut(self.own, i), self.cut(self.early, i), s1.at[i], r1.at[i], self.place.chip_z(mate))

    def across(self, i):
        s2, r2 = self.sems[2:4]
        return remote(self.cut(self.mid, i), self.cut(self.low, i), s2.at[i], r2.at[i], self.place.chip_z(3 - self.place.t))

    def back(self, i, mate):
        s3, r3 = self.sems[4:6]
        return remote(self.cut(self.total, i), self.cut(self.total, i), s3.at[i], r3.at[i], self.place.chip_z(mate))

    def send(self, i):
        @pl.when(self.place.outer)
        def _():
            self.from_end(i, self.place.inner_mate).start()

    def pair_up(self, i):
        @pl.when(jnp.logical_not(self.place.outer))
        def _():
            self.from_end(i, self.place.outer_mate).wait_recv()
            pair = self.cut(self.own, i)[...].astype(jnp.float32) + self.cut(self.early, i)[...].astype(jnp.float32)
            self.cut(self.mid, i)[...] = pair.astype(self.mid.dtype)
            self.across(i).start()

    def join(self, i):
        @pl.when(jnp.logical_not(self.place.outer))
        def _():
            self.across(i).wait_recv()
            whole = self.cut(self.mid, i)[...].astype(jnp.float32) + self.cut(self.low, i)[...].astype(jnp.float32)
            self.cut(self.total, i)[...] = whole.astype(self.total.dtype)
            self.back(i, self.place.outer_mate).start()

    def receive(self, i):
        @pl.when(self.place.outer)
        def _():
            self.back(i, self.place.inner_mate).wait_recv()

    def finish(self, pieces):
        @pl.when(self.place.outer)
        def _():
            for i in range(pieces):
                self.from_end(i, self.place.inner_mate).wait_send()

        @pl.when(jnp.logical_not(self.place.outer))
        def _():
            for i in range(pieces):
                self.across(i).wait_send()
                self.back(i, self.place.outer_mate).wait_send()


def nt_dot(left, right):
    return lax.dot_general(left, right, (((1,), (1,)), ((), ())), preferred_element_type=jnp.float32)


def nn_dot(left, right):
    return jnp.dot(left, right, preferred_element_type=jnp.float32)


def tn_dot(left, right):
    return lax.dot_general(left, right, (((0,), (0,)), ((), ())), preferred_element_type=jnp.float32)


def centred(values):
    centre = values - jnp.mean(values, axis=-1, keepdims=True)
    spread = jnp.mean(centre * centre, axis=-1, keepdims=True)
    return centre, lax.rsqrt(spread + norm_eps)


def norm_back(values, gain_row, grads):
    centre, scale = centred(values)
    xhat = centre * scale
    e = grads * gain_row
    moved = scale * (e - jnp.mean(e, axis=-1, keepdims=True) - xhat * jnp.mean(e * xhat, axis=-1, keepdims=True))
    return moved, jnp.sum(grads * xhat, axis=0, keepdims=True)


def layer_both_ways(tokens, out_grad, own_block, norm_gains, cosine, sine, seg_column, seg_row, counts, ident):
    count, width = tokens.shape
    local_rows = own_block.shape[0]
    inner = counts[1]
    ff = counts[3]
    heads = inner // HEAD_DIM
    full = 2 * count
    rows = count // 4
    sub = rows // 2
    stack = heads * rows
    piece = 64
    score_scale = HEAD_DIM ** (-0.5)
    f32, low = jnp.float32, jnp.bfloat16
    first_plan, first_count = gather_plan(counts, local_rows, (0, 1), 64)
    last_plan, last_count = gather_plan(counts, local_rows, (2, 3), 64)
    first_base, first_rows = base_rows(counts, (0, 1))
    last_base, last_rows = base_rows(counts, (2, 3))

    def kernel(tok_ref, og_ref, own_ref, gain_ref, cos_ref, sin_ref, sc_ref, sr_ref,
               act_ref, attn_ref, resid_ref, mlp_ref, hid_ref, dm_ref, b2_ref, dres_ref, db_ref, dproj_ref, t3_ref, dg_ref,
               w1st, wlast, q_ref, kv_ref, kq_ref, p_ref, s_ref, pl_ref, do_ref, dp_ref, ds_ref,
               t1_ref, e1, m1, l1, sum1, t2_ref, e2, m2, l2, sum2, dq_ref, dkv_ref, dkv_tx, dkv_rx, *sems):
        place = Place()
        greet(place, True, True, True)
        begin1, steps1, ready1, end1 = gather_steps(place, first_plan, local_rows, first_base, own_ref, w1st, sems[0:4], 1)
        begin2, steps2, ready2, end2 = gather_steps(place, last_plan, local_rows, last_base, own_ref, wlast, sems[4:8])
        line1 = LineSum(place, sub, t1_ref, e1, m1, l1, sum1, sems[8:14])
        line2 = LineSum(place, sub, t2_ref, e2, m2, l2, sum2, sems[14:20])
        swap, local_sem = sems[20], sems[21]

        begin1()
        own_rows_copy(place, counts, local_rows, (0, 1), first_base, own_ref, w1st, local_sem, lambda d: d.start())

        def at(i, size=rows):
            return pl.ds(pl.multiple_of(i * size, size), size)

        def norm_one(i, carry):
            centre, scale = centred(tok_ref[at(i)].astype(f32))
            act_ref[at(i)] = (centre * scale * gain_ref[0:1]).astype(low)
            return carry

        lax.fori_loop(0, 4, norm_one, 0)
        dg_ref[...] = jnp.zeros_like(dg_ref)
        begin2()
        run_steps(steps1)
        own_rows_copy(place, counts, local_rows, (0, 1), first_base, own_ref, w1st, local_sem, lambda d: d.wait())
        own_rows_copy(place, counts, local_rows, (2, 3), last_base, own_ref, wlast, local_sem, lambda d: d.start())
        ready1()
        waiting = list(steps2)

        def forward(number):
            for step in waiting[:number]:
                step()
            del waiting[:number]

        forward(1)

        lane = lax.broadcasted_iota(jnp.int32, (1, inner), 1)
        front = (lane % HEAD_DIM) < HEAD_DIM // 2

        def half_turn(value):
            return jnp.where(front, pltpu.roll(value, inner - HEAD_DIM // 2, 1), pltpu.roll(value, HEAD_DIM // 2, 1))

        sign = jnp.where(front, -1.0, 1.0).astype(f32)

        def rotated(value, i):
            return value * cos_ref[at(i)] + half_turn(value) * (sin_ref[at(i)] * sign)

        def rotated_back(value, i):
            return value * cos_ref[at(i)] - half_turn(value * sin_ref[at(i)]) * sign

        def project_rows(i, carry):
            value = nt_dot(act_ref[at(i)], w1st[0:3 * inner])
            q_ref[at(i)] = rotated(value[:, 0:inner], i).astype(low)
            kv_ref[at(i), 0:inner] = rotated(value[:, inner:2 * inner], i).astype(low)
            kv_ref[at(i), inner:2 * inner] = value[:, 2 * inner:3 * inner].astype(low)
            return carry

        lax.fori_loop(0, 4, project_rows, 0)
        kv_copy = remote(kv_ref.at[pl.ds(0, count)], kv_ref.at[pl.ds(count, count)], swap.at[0], swap.at[1], place.partner())
        kv_copy.start()
        forward(2)
        kv_copy.wait()

        def head_mask(h):
            return jnp.logical_and(lane >= h * HEAD_DIM, lane < (h + 1) * HEAD_DIM)

        def stacked(value):
            return jnp.concatenate([jnp.where(head_mask(h), value, jnp.zeros_like(value)) for h in range(heads)], axis=0)

        def unstacked(value):
            total = jnp.where(head_mask(0), value[0:rows], 0.0)
            for h in range(1, heads):
                total = total + jnp.where(head_mask(h), value[h * rows:(h + 1) * rows], 0.0)
            return total

        per = rows // piece

        def attend(i):
            kq_ref[...] = stacked(q_ref[at(i)])
            s_ref[...] = nt_dot(kq_ref[...], kv_ref[:, 0:inner])

            def soft(r, inside):
                seg = sc_ref[pl.ds(pl.multiple_of(i * rows + (r % per) * piece, piece), piece)]
                score = jnp.where(seg == sr_ref[...], s_ref[at(r, piece)] * score_scale, -jnp.inf)
                score = jnp.exp(score - jnp.max(score, axis=-1, keepdims=True))
                prob = score * (1.0 / jnp.sum(score, axis=-1, keepdims=True))
                p_ref[i, at(r, piece)] = prob
                pl_ref[at(r, piece)] = prob.astype(low)
                return inside

            lax.fori_loop(0, stack // piece, soft, 0)
            mixed = unstacked(nn_dot(pl_ref[...], kv_ref[:, inner:2 * inner]))
            keep = (sc_ref[at(i)] > 0).astype(f32)
            attn = (mixed * keep).astype(low)
            attn_ref[at(i)] = attn
            t1_ref[at(i)] = nn_dot(attn, w1st[3 * inner:4 * inner]).astype(low)
            for part in range(2):
                line1.send(2 * i + part)

            if i >= 1:
                line1.pair_up(2 * i - 2)
                line1.pair_up(2 * i - 1)
            if i >= 2:
                line1.join(2 * i - 4)
                line1.join(2 * i - 3)

        for i in range(4):
            attend(i)
            forward(2)
        forward(len(waiting))
        own_rows_copy(place, counts, local_rows, (2, 3), last_base, own_ref, wlast, local_sem, lambda d: d.wait())
        ready2()

        def feed(i, carry):
            for part in range(2):
                line1.receive(2 * i + part)
            resid = tok_ref[at(i)].astype(f32) + sum1[at(i)].astype(f32)
            resid_ref[at(i)] = resid
            centre, scale = centred(resid)
            mlp = (centre * scale * gain_ref[1:2]).astype(low)
            mlp_ref[at(i)] = mlp
            gate = nt_dot(mlp, wlast[0:ff])
            up = nt_dot(mlp, wlast[ff:2 * ff])
            cdf = 0.5 * (1.0 + lax.erf(gate * (0.5 ** 0.5)))
            bell = jnp.exp(gate * gate * -0.5) * (1.0 / math.sqrt(2.0 * math.pi))
            gelu = gate * cdf
            hidden = (gelu * up).astype(low)
            hid_ref[at(i)] = hidden
            dhidden = nt_dot(og_ref[at(i)], wlast[2 * ff:3 * ff])
            dgate = (dhidden * up * (cdf + gate * bell)).astype(low)
            dup = (dhidden * gelu).astype(low)
            dm_ref[0, at(i)] = dgate
            dm_ref[1, at(i)] = dup
            t2_ref[at(i)] = (nn_dot(dgate, wlast[0:ff]) + nn_dot(dup, wlast[ff:2 * ff])).astype(low)
            for part in range(2):
                line2.send(2 * i + part)
            b2_ref[at(i)] = nn_dot(hidden, wlast[2 * ff:3 * ff]).astype(low)

            @pl.when(i == 0)
            def _():
                line1.pair_up(6)
                line1.pair_up(7)

            @pl.when(i <= 1)
            def _():
                line1.join(2 * i + 4)
                line1.join(2 * i + 5)

            @pl.when(i >= 1)
            def _():
                line2.pair_up(2 * i - 2)
                line2.pair_up(2 * i - 1)

            @pl.when(i >= 2)
            def _():
                line2.join(2 * i - 4)
                line2.join(2 * i - 3)
            return carry

        lax.fori_loop(0, 4, feed, 0)
        dkv_ref[...] = jnp.zeros_like(dkv_ref)

        def turn_back(i, carry):
            @pl.when(i == 0)
            def _():
                line2.pair_up(6)
                line2.pair_up(7)
            for part in range(2):
                line2.receive(2 * i + part)
            moved, gain_part = norm_back(resid_ref[at(i)], gain_ref[1:2], sum2[at(i)].astype(f32))
            dg_ref[1:2] = dg_ref[1:2] + gain_part
            dresid = og_ref[at(i)].astype(f32) + moved
            dres_ref[at(i)] = dresid
            dbranch = dresid.astype(low)
            db_ref[at(i)] = dbranch
            keep = (sc_ref[at(i)] > 0).astype(low)
            dattn = nt_dot(dbranch, w1st[3 * inner:4 * inner]).astype(low) * keep
            do_ref[...] = stacked(dattn)
            kq_ref[...] = stacked(q_ref[at(i)])
            dp_ref[...] = nt_dot(do_ref[...], kv_ref[:, inner:2 * inner])

            def soft_back(r, inside):
                prob = p_ref[i, at(r, piece)]
                dprob = dp_ref[at(r, piece)]
                delta = jnp.sum(prob * dprob, axis=-1, keepdims=True)
                ds_ref[at(r, piece)] = (prob * (dprob - delta) * score_scale).astype(low)
                pl_ref[at(r, piece)] = prob.astype(low)
                return inside

            lax.fori_loop(0, stack // piece, soft_back, 0)
            dq_ref[at(i)] = unstacked(nn_dot(ds_ref[...], kv_ref[:, 0:inner]))
            dkv_ref[:, 0:inner] = dkv_ref[:, 0:inner] + tn_dot(ds_ref[...], kq_ref[...])
            dkv_ref[:, inner:2 * inner] = dkv_ref[:, inner:2 * inner] + tn_dot(pl_ref[...], do_ref[...])

            @pl.when(i <= 1)
            def _():
                line2.join(2 * i + 4)
                line2.join(2 * i + 5)
            return carry

        lax.fori_loop(0, 4, turn_back, 0)
        dkv_tx[...] = dkv_ref[count:full].astype(low)
        dkv_copy = remote(dkv_tx, dkv_rx, swap.at[2], swap.at[3], place.partner())
        dkv_copy.start()

        def unproject_query(i, carry):
            dproj_ref[at(i), 0:inner] = rotated_back(dq_ref[at(i)], i).astype(low)
            return carry

        lax.fori_loop(0, 4, unproject_query, 0)
        dkv_copy.wait()

        def unproject(i, carry):
            both = dkv_ref[at(i)] + dkv_rx[at(i)].astype(f32)
            dproj_ref[at(i), inner:2 * inner] = rotated_back(both[:, 0:inner], i).astype(low)
            dproj_ref[at(i), 2 * inner:3 * inner] = both[:, inner:2 * inner].astype(low)
            t3_ref[at(i)] = nn_dot(dproj_ref[at(i)], w1st[0:3 * inner]).astype(low)
            return carry

        lax.fori_loop(0, 4, unproject, 0)
        line1.finish(8)
        line2.finish(8)
        end1()
        end2()

    def shape(*dims, dtype=low):
        return jax.ShapeDtypeStruct(dims, dtype)

    outs = (
        shape(count, width), shape(count, inner), shape(count, width, dtype=f32), shape(count, width), shape(count, ff),
        shape(2, count, ff), shape(count, width), shape(count, width, dtype=f32), shape(count, width),
        shape(count, 3 * inner), shape(count, width), shape(8, width, dtype=f32),
    )
    line = pltpu.VMEM((count, width), low)
    scratch = [
        pltpu.VMEM((first_rows, width), low), pltpu.VMEM((last_rows, width), low), pltpu.VMEM((count, inner), low),
        pltpu.VMEM((full, 2 * inner), low), pltpu.VMEM((stack, inner), low), pltpu.VMEM((4, stack, full), f32),
        pltpu.VMEM((stack, full), f32), pltpu.VMEM((stack, full), low), pltpu.VMEM((stack, inner), low),
        pltpu.VMEM((stack, full), f32), pltpu.VMEM((stack, full), low),
    ]
    scratch += [line] * 10
    scratch += [
        pltpu.VMEM((count, inner), f32), pltpu.VMEM((full, 2 * inner), f32),
        pltpu.VMEM((count, 2 * inner), low), pltpu.VMEM((count, 2 * inner), low),
    ]
    scratch += [dma(first_count)] * 4 + [dma(last_count)] * 4 + [dma(8)] * 12 + [dma(4), dma(1)]
    ins = (tokens, out_grad, own_block, norm_gains, cosine, sine, seg_column, seg_row)
    return pl.pallas_call(
        kernel,
        out_shape=outs,
        in_specs=[VMEM_SPEC] * len(ins),
        out_specs=(VMEM_SPEC,) * len(outs),
        scratch_shapes=scratch,
        compiler_params=pltpu.CompilerParams(
            collective_id=ident, has_side_effects=True, vmem_limit_bytes=67043328
        ),
    )(*ins)


def tail_grams(left_right, muon_rows, counts, ident):
    dproj, act_in, attn_in, dbranch, dmixed, mlp_in, hidden, out_low = left_right
    local_rows, width = muon_rows.shape
    ks = (0, 1, 2, 3)
    plan, count = gather_plan(counts, local_rows, ks, 96)
    base, total_rows = base_rows(counts, ks)
    ff = counts[3]
    tile = width // 4
    half = tile // 2
    chunks = 10
    f32, low16 = jnp.float32, jnp.bfloat16

    def kernel(dp_ref, act_ref, at_ref, db_ref, dm_ref, mlp_ref, hid_ref, og_ref, mu_ref,
               grad_ref, next_ref, x_ref, g_ref, norm_ref,
               part, prx, rrx, mine, theirs, gprx, tot, other, early, mid, low, norm_own, *sems):
        place = Place()
        c = place.c
        greet(place, True, True, True)
        begin, steps, end = scatter_steps(place, plan, local_rows, base, part, grad_ref, prx, rrx, part, sems[:4])

        def terms(row, left, right):
            span = left.shape[1]

            def columns(j, carry):
                cols = pl.ds(pl.multiple_of(j * tile, tile), tile)
                part[pl.ds(row, span), cols] = tn_dot(left[...], right[:, cols]).astype(low16)
                return carry

            lax.fori_loop(0, 4, columns, 0)

        terms(base[2], dm_ref.at[0], mlp_ref)
        terms(base[2] + ff, dm_ref.at[1], mlp_ref)
        begin((2,))
        terms(base[3], hid_ref, og_ref)
        begin((3,))
        terms(base[0], dp_ref, act_ref)
        begin((0,))
        terms(base[1], at_ref, db_ref)
        begin((1,))
        grad_ref[...] = jnp.zeros_like(grad_ref)
        run_steps(steps)
        end()

        def momentum(i, carry):
            sl = pl.ds(pl.multiple_of(i * 16, 16), 16)
            grad = grad_ref[sl]
            after = muon_beta * mu_ref[sl] + (1.0 - muon_beta) * grad
            next_ref[sl] = after
            direction = (1.0 - muon_beta) * grad + muon_beta * after
            x_ref[sl] = direction.astype(low16)
            square = direction * direction
            return carry + square[0:8] + square[8:16]

        square = lax.fori_loop(0, local_rows // 16, momentum, jnp.zeros((8, width), f32))
        own_square = jnp.broadcast_to(jnp.sum(jnp.sum(square, axis=1, keepdims=True), axis=0, keepdims=True), (8, tile))
        norm_own[...] = own_square

        sp, rp, st, rt = sems[10:14]

        def blocks(core):
            return [(3 * core, 3 * core), (2 * core, 2 * core + 1), (core + 1, core + 1), (core, core + 2), (core, 3 - core)]

        def at(k):
            return pl.ds(pl.multiple_of(k * tile, tile), tile)

        def gram(i, j):
            return tn_dot(x_ref[:, at(i)], x_ref[:, at(j)])

        def partner(n):
            sl = pl.ds(n * tile, tile)
            return remote(theirs.at[sl], gprx.at[sl], sp.at[n], rp.at[n], place.partner())

        def norm_row(ref):
            return ref.at[pl.ds(5 * tile, 8)]

        for n, (i, j) in enumerate(blocks(1 - c)):
            theirs[pl.ds(n * tile, tile)] = gram(i, j)
            partner(n).start()
        norm_row(theirs)[...] = norm_own[...]
        pn = remote(norm_row(theirs), norm_row(gprx), sp.at[5], rp.at[5], place.partner())
        pn.start()

        def span(i):
            return pl.ds(i * half, half) if i < chunks - 1 else pl.ds(i * half, half + 8)

        def cut(ref):
            return lambda i: ref.at[span(i)]

        def prep(i):
            if i % 2 == 0:
                n = i // 2
                sl = pl.ds(n * tile, tile)
                block = gram(*blocks(c)[n])
                partner(n).wait_recv()
                mine[sl] = block + gprx[sl]
            if i == chunks - 1:
                pn.wait_recv()
                norm_row(mine)[...] = norm_row(gprx)[...] + norm_own[...]

        def share(i):
            return remote(cut(tot)(i), cut(other)(i), st.at[i], rt.at[i], place.partner())

        def place_block(ref, n, core):
            i, j = blocks(core)[n]
            block = ref[pl.ds(n * tile, tile)]
            g_ref[at(i), at(j)] = block
            g_ref[at(j), at(i)] = block.T

        def done(i):
            share(i).start()
            if i % 2 == 1:
                place_block(tot, i // 2, c)
            if i >= 2:
                share(i - 2).wait_recv()
                if (i - 2) % 2 == 1:
                    place_block(other, (i - 2) // 2, 1 - c)

        line, line_end = line_steps(place, chunks, cut(mine), cut(tot), cut(early), cut(mid), cut(low), sems[4:10],
                                    prep=prep, done=done)
        run_steps(line)
        for i in (chunks - 2, chunks - 1):
            share(i).wait_recv()
        place_block(other, 4, 1 - c)
        norm_ref[...] = jnp.broadcast_to(tot[5 * tile:5 * tile + 8, 0:128], (8, 128))
        line_end()
        for n in range(5):
            partner(n).wait_send()
        pn.wait_send()
        for i in range(chunks):
            share(i).wait_send()

    rows_low = pltpu.VMEM((total_rows, width), low16)
    packed = pltpu.VMEM((5 * tile + 8, tile), f32)
    outs = (
        jax.ShapeDtypeStruct((local_rows, width), f32), jax.ShapeDtypeStruct((local_rows, width), f32),
        jax.ShapeDtypeStruct((local_rows, width), low16), jax.ShapeDtypeStruct((width, width), f32),
        jax.ShapeDtypeStruct((8, 128), f32),
    )
    scratch = [rows_low] * 3 + [packed] * 8 + [pltpu.VMEM((8, tile), f32)]
    scratch += [dma(count)] * 4 + [dma(chunks)] * 6 + [dma(6), dma(6), dma(chunks), dma(chunks)]
    ins = tuple(left_right) + (muon_rows,)
    return comm_call(kernel, outs, ins, [VMEM_SPEC] * len(ins), (VMEM_SPEC,) * len(outs), scratch, ident)


def halves(value):
    high = value.astype(jnp.bfloat16)
    return high, (value - high.astype(jnp.float32)).astype(jnp.bfloat16)


def iterate(gram, norm, direction_low, own_block, normed_term, branch_term, tokens_in, resid, dresid, dgain_rows, norm_gains, adam_first,
            adam_second, ident):
    rows, width = direction_low.shape
    tile = 256
    parts = width // tile
    tokens = branch_term.shape[0]
    each = 8
    chunks = 2 * each
    step_rows = tokens // each
    aa = ns_first * ns_first
    ab = 2.0 * ns_first * ns_second
    bbac = ns_second * ns_second + 2.0 * ns_first * ns_third
    bc = 2.0 * ns_second * ns_third
    cc = ns_third * ns_third
    correction = 1.0 - adam_beta**STEP

    def kernel(g_ref, n_ref, d_ref, w_ref, t3_ref, b2_ref, tok_ref, r_ref, dres_ref, dgr_ref, gain_ref, af_ref, as_ref,
               u_ref, lo_ref, tg_ref, gg_ref, afn_ref, asn_ref, gu_ref,
               p_ref, ph, pl_, hh, hl, uh, ul, mx, x_ref, early, mid, low, total, held, dg_ref, *sems):
        place = Place()
        s1, r1, s2, r2, s3, r3, sg, rg = sems
        me = place.f * 2 + place.c
        barrier = pltpu.get_barrier_semaphore()

        def plane(shift):
            other = (me + shift) % 8
            return (other // 2, other % 2, place.t)

        for shift in range(1, 8):
            pl.semaphore_signal(barrier, inc=1, device_id=plane(shift), device_id_type=MESH_ID)

        @pl.when(place.outer)
        def _():
            pl.semaphore_signal(barrier, inc=1, device_id=place.chip_z(place.inner_mate), device_id_type=MESH_ID)
            pl.semaphore_wait(barrier, 8)

        @pl.when(jnp.logical_not(place.outer))
        def _():
            pl.semaphore_signal(barrier, inc=1, device_id=place.chip_z(place.outer_mate), device_id_type=MESH_ID)
            pl.semaphore_signal(barrier, inc=1, device_id=place.chip_z(3 - place.t), device_id_type=MESH_ID)
            pl.semaphore_wait(barrier, 9)

        def cut(ref, i):
            if isinstance(i, int):
                return ref.at[pl.ds(i * step_rows, step_rows)]
            return ref.at[pl.ds(pl.multiple_of(i * step_rows, step_rows), step_rows)]

        def from_end(i, device, own):
            local = i % each
            return remote(cut(own, local), cut(early, i), s1.at[i], r1.at[i], device)

        def across(i):
            return remote(cut(mid, i), cut(low, i), s2.at[i], r2.at[i], place.chip_z(3 - place.t))

        def back(i, device):
            return remote(cut(total, i), cut(total, i), s3.at[i], r3.at[i], device)

        dg_ref[...] = jnp.zeros_like(dg_ref)

        @pl.when(place.outer)
        def _():
            for i in range(each):
                from_end(i, place.chip_z(place.inner_mate), t3_ref).start()
            for i in range(each):
                from_end(each + i, place.chip_z(place.inner_mate), b2_ref).start()

        def pair_up(i, own):
            @pl.when(jnp.logical_not(place.outer))
            def _():
                from_end(i, place.chip_z(place.outer_mate), own).wait_recv()
                pair = cut(own, i % each)[...].astype(jnp.float32) + cut(early, i)[...].astype(jnp.float32)
                cut(mid, i)[...] = pair.astype(mid.dtype)
                across(i).start()

        def pair_some(first):
            for part in range(4):
                @pl.when(first + part < each)
                def _():
                    pair_up(first + part, t3_ref)

                @pl.when(first + part >= each)
                def _():
                    pair_up(first + part, b2_ref)

        def join_some(first):
            for part in range(2):
                join(first + part)

        def join(i):
            @pl.when(jnp.logical_not(place.outer))
            def _():
                across(i).wait_recv()
                whole = cut(mid, i)[...].astype(jnp.float32) + cut(low, i)[...].astype(jnp.float32)
                cut(total, i)[...] = whole.astype(total.dtype)
                back(i, place.chip_z(place.outer_mate)).start()

        norm_size = jnp.sqrt(n_ref[0:1, 0:1])
        inverse = 1.0 / (norm_size + ortho_eps)
        scale = inverse * inverse

        for k in range(parts):
            sl = pl.ds(k * tile, tile)
            value = g_ref[sl] * scale
            p_ref[sl] = value
            high, rest = halves(value)
            ph[sl] = high
            pl_[sl] = rest
        x_ref[...] = d_ref[...].astype(jnp.float32) * inverse

        def product(lh, ll, rh, rl, k):
            sl, cols = pl.ds(k * tile, tile), pl.ds(k * tile, width - k * tile)

            def dot(left, right):
                return jnp.dot(left[sl], right[:, cols], preferred_element_type=jnp.float32)

            return dot(lh, rh) + dot(ll, rh) + dot(lh, rl)

        def spread_out(value, high_ref, low_ref, k):
            sl, cols = pl.ds(k * tile, tile), pl.ds(k * tile, width - k * tile)
            high, rest = halves(value)
            high_ref[sl, cols] = high
            low_ref[sl, cols] = rest
            for j in range(k + 1, parts):
                at = (j - k) * tile
                high_ref[pl.ds(j * tile, tile), sl] = high[:, at:at + tile].T
                low_ref[pl.ds(j * tile, tile), sl] = rest[:, at:at + tile].T

        def squares():
            for k in range(parts):
                sl, cols = pl.ds(k * tile, tile), pl.ds(k * tile, width - k * tile)
                value = product(ph, pl_, ph, pl_, k)
                spread_out(value, hh, hl, k)
                mix = (ns_second * p_ref[sl, cols] + ns_third * value).astype(mx.dtype)
                mx[sl, cols] = mix
                for j in range(k + 1, parts):
                    at = (j - k) * tile
                    mx[pl.ds(j * tile, tile), sl] = mix[:, at:at + tile].T

        def rotate_rows():
            for at, size in ((0, 336), (336, 320)):
                sl = pl.ds(at, size)
                old = x_ref[sl]
                x_ref[sl] = ns_first * old + jnp.dot(old.astype(jnp.bfloat16), mx[...], preferred_element_type=jnp.float32)

        def gains_copy(shift):
            return remote(dg_ref, held.at[me], sg.at[shift], rg.at[shift], plane(shift))

        def first_norm_back():
            @pl.when(place.outer)
            def _():
                for i in range(each):
                    back(i, place.chip_z(place.inner_mate)).wait_recv()

            def some(i, inside):
                sl = pl.ds(pl.multiple_of(i * 64, 64), 64)
                moved, gain_part = norm_back(tok_ref[sl].astype(jnp.float32), gain_ref[0:1], total[sl].astype(jnp.float32))
                dg_ref[0:1] = dg_ref[0:1] + gain_part
                tg_ref[sl] = (dres_ref[sl] + moved).astype(tg_ref.dtype)
                return inside

            lax.fori_loop(0, tokens // 64, some, 0)
            dg_ref[1:2] = dgr_ref[1:2]
            held[pl.ds(me, 1)] = dg_ref[...][None]
            for shift in range(1, 8):
                gains_copy(shift).start()

        def body(sweep, carry):
            @pl.when(sweep >= 1)
            def _():
                join_some(4 * sweep - 4)
            squares()

            @pl.when(sweep >= 1)
            def _():
                join_some(4 * sweep - 2)
            rotate_rows()

            @pl.when(sweep < ITERS - 1)
            def _():
                for k in range(parts):
                    sl, cols = pl.ds(k * tile, tile), pl.ds(k * tile, width - k * tile)
                    cube = product(ph, pl_, hh, hl, k)
                    square = hh[sl, cols].astype(jnp.float32) + hl[sl, cols].astype(jnp.float32)
                    spread_out(bc * square + cc * cube, uh, ul, k)
                    p_ref[sl, cols] = aa * p_ref[sl, cols] + ab * square + bbac * cube

                pair_some(4 * sweep)
                for k in range(parts):
                    sl, cols = pl.ds(k * tile, tile), pl.ds(k * tile, width - k * tile)
                    value = p_ref[sl, cols] + product(hh, hl, uh, ul, k)
                    p_ref[sl, cols] = value
                    spread_out(value, ph, pl_, k)

            @pl.when(sweep == ITERS - 2)
            def _():
                first_norm_back()
            return carry

        lax.fori_loop(0, ITERS, body, 0)
        spread = jnp.where(place.f == 0, 0.2 * math.sqrt(3 * D), jnp.where(place.f == 1, 0.2 * math.sqrt(D), jnp.where(
            place.f == 2, 0.2 * math.sqrt(2 * FF), 0.2 * math.sqrt(FF)))).astype(jnp.float32)
        u_ref[...] = -muon_rate * (spread * x_ref[...] + decay_rate * w_ref[...].astype(jnp.float32))

        for shift in range(1, 8):
            gains_copy(shift).wait()
        grads = held[0]
        for k in range(1, 8):
            grads = grads + held[k]
        grads = grads[0:2]
        gg_ref[...] = grads
        first = adam_beta * af_ref[...] + (1.0 - adam_beta) * grads
        second = adam_beta * as_ref[...] + (1.0 - adam_beta) * grads * grads
        afn_ref[...] = first
        asn_ref[...] = second
        gu_ref[...] = -adam_rate * (
            first / correction / (jnp.sqrt(second / correction) + adam_eps) + decay_rate * gain_ref[...]
        )

        @pl.when(place.outer)
        def _():
            for i in range(each, chunks):
                back(i, place.chip_z(place.inner_mate)).wait_recv()
            for i in range(each):
                from_end(i, place.chip_z(place.inner_mate), t3_ref).wait_send()
                from_end(each + i, place.chip_z(place.inner_mate), b2_ref).wait_send()
        lo_ref[...] = (r_ref[...] + total[tokens:2 * tokens].astype(jnp.float32)).astype(lo_ref.dtype)

        @pl.when(jnp.logical_not(place.outer))
        def _():
            for i in range(chunks):
                across(i).wait_send()
                back(i, place.chip_z(place.outer_mate)).wait_send()

    f32, low16 = jnp.float32, jnp.bfloat16
    small = jax.ShapeDtypeStruct(norm_gains.shape, f32)
    narrow = jax.ShapeDtypeStruct((tokens, width), low16)
    outs = (jax.ShapeDtypeStruct((rows, width), f32), narrow, narrow, small, small, small, small)
    full = pltpu.VMEM((width, width), low16)
    line = pltpu.VMEM((2 * tokens, width), low16)
    scratch = [pltpu.VMEM((width, width), f32)] + [full] * 7 + [pltpu.VMEM((rows, width), f32)] + [line] * 4
    scratch += [pltpu.VMEM((8, 8, width), f32), pltpu.VMEM((8, width), f32)] + [dma(chunks)] * 6 + [dma(8)] * 2
    ins = (gram, norm, direction_low, own_block, normed_term, branch_term, tokens_in, resid, dresid, dgain_rows, norm_gains,
           adam_first, adam_second)
    return comm_call(kernel, outs, ins, [VMEM_SPEC] * len(ins), (VMEM_SPEC,) * len(outs), scratch, ident)


def per_device_block(tokens, out_grad, weight_stack, muon_state, norm_gains, adam_first, adam_second, segment_ids,
                     position_ids):
    token_count, _, model_width = tokens.shape
    groups, contexts = 4, 2
    full_len = token_count * contexts
    local_rows = weight_stack.shape[2]
    heads_dev = HEADS // groups
    ff_dev = FF // groups
    inner_width = heads_dev * HEAD_DIM
    counts = (3 * inner_width, inner_width, 2 * ff_dev, ff_dev)
    own_block = weight_stack.reshape(local_rows, model_width)
    context = lax.axis_index("context")

    cosine, sine_table = rope_tables(position_ids.reshape(token_count), HEAD_DIM)
    segments = segment_ids.reshape(full_len)
    seg_query = lax.dynamic_slice_in_dim(segments, context * token_count, token_count, 0)
    seg_other = lax.dynamic_slice_in_dim(segments, (1 - context) * token_count, token_count, 0)
    (act_in, attn_in, resid, mlp_in, hidden, dmixed, branch_two_term, dresid, dbranch_one, dprojected, dnormed_one_term,
     dgain_rows) = layer_both_ways(
        tokens.reshape(token_count, model_width), out_grad.reshape(token_count, model_width), own_block, norm_gains,
        jnp.tile(cosine, (1, heads_dev)), jnp.tile(sine_table, (1, heads_dev)),
        seg_query.reshape(token_count, 1), jnp.concatenate([seg_query, seg_other]).reshape(1, full_len), counts, 0,
    )
    grad_block, muon_next, direction_low, gram, norm_total = tail_grams(
        (dprojected, act_in, attn_in, dbranch_one, dmixed, mlp_in, hidden, out_grad.reshape(token_count, model_width)),
        muon_state.reshape(local_rows, model_width), counts, 1,
    )
    direction_scale = jnp.log(jnp.sqrt(norm_total[0, 0])).reshape(1)
    weight_update, layer_out, tokens_grad, gain_grads, adam_first_next, adam_second_next, gain_update = iterate(
        gram, norm_total, direction_low, own_block, dnormed_one_term, branch_two_term,
        tokens.reshape(token_count, model_width), resid, dresid, dgain_rows, norm_gains, adam_first, adam_second, 2,
    )
    layer_out = layer_out.reshape(tokens.shape)
    tokens_grad = tokens_grad.reshape(tokens.shape)
    block_shape = (1, 1, local_rows, model_width)
    return (
        layer_out,
        tokens_grad,
        grad_block.reshape(block_shape),
        muon_next.reshape(block_shape),
        weight_update.reshape(block_shape),
        direction_scale,
        gain_grads,
        adam_first_next,
        adam_second_next,
        gain_update,
    )


def solution(mesh):
    sizes = dict(mesh.shape)
    block = (sizes["fsdp"], sizes["context"], sizes["tensor"]) == (4, 2, 4)
    return jax.shard_map(
        per_device_block if block else per_device,
        mesh=mesh,
        in_specs=(
            P("context", "fsdp", None),
            P("context", "fsdp", None),
            P("fsdp", "tensor", "context", None),
            P("fsdp", "tensor", "context", None),
            P(),
            P(),
            P(),
            P(None, "fsdp"),
            P("context", "fsdp"),
        ),
        out_specs=(
            P("context", "fsdp", None),
            P("context", "fsdp", None),
            P("fsdp", "tensor", "context", None),
            P("fsdp", "tensor", "context", None),
            P("fsdp", "tensor", "context", None),
            P("fsdp"),
            P(),
            P(),
            P(),
            P(),
        ),
        check_vma=False,
    )
```

profile of v0, /device:TPU:0, one launch (start us, length us, event | category | flops | bytes accessed | tf_op | source)
XLA Modules:
  0.0 345.4 jit_solution(14026029279956504100)
XLA Ops:
  0.7 0.7 convert_element_type.4
  1.3 0.7 constant_dynamic-slice_fusion
  2.0 0.6 pad_add_fusion
  2.6 0.1 broadcast_multiply_fusion
  2.7 0.2 fusion
  3.0 0.9 copy.23.sc_ref
  3.9 1.0 copy.22.sin_ref
  4.9 1.0 copy.21.cos_ref
  5.9 126.5 %shard_map.168 = (bf16[512,1024]{1,0:T(8,128)(2,1)}, bf16[512,256]{1,0:T(8,128)(2,1)}, f32[512,1024]{1,0:T(8,128)}, bf16[512,1024]{1,0:T(8,128)(2,1)}, bf16[512,...) custom-call(bf16[512,1024]{1,0:T(8,128)(2,1)} %bitcast.20, ...), custom_call_target="tpu_custom_call" | custom-call | tf_op jit(solution)/shard_map/pallas_call | solution.py:1025
  132.5 95.5 %shard_map.169 = (f32[656,1024]{1,0:T(8,128)}, f32[656,1024]{1,0:T(8,128)}, bf16[656,1024]{1,0:T(8,128)(2,1)}, f32[1024,1024]{1,0:T(8,128)}, f32[8,128]{1,0:T(8,128)}) custom-call(bf16[512,768]{1,0:T(8,128)(2,1)} %get-tuple-element.34.dp_ref, bf16[512,1024]{1,0:T(8,128)(2,1)} %get-tuple-element.35.act_ref, bf16[512,256]{1,0:T(8,128)(2,1)} %get-tuple-element.36.at_ref, ...), custom_call_target="tpu_custom_call" | custom-call | tf_op jit(solution)/shard_map/pallas_call | solution.py:637
  228.0 1.2 slice.3
  229.9 100.2 %shard_map.170 = (f32[656,1024]{1,0:T(8,128)}, bf16[512,1024]{1,0:T(8,128)(2,1)}, bf16[512,1024]{1,0:T(8,128)(2,1)}, f32[2,1024]{1,0:T(2,128)}, f32[2,1024]{1,0:...) custom-call(f32[1024,1024]{1,0:T(8,128)} %get-tuple-element.41.g_ref, f32[8,128]{1,0:T(8,128)} %get-tuple-element.42.n_ref, ...), custom_call_target="tpu_custom_call" | custom-call | tf_op jit(solution)/shard_map/pallas_call | solution.py:637
  330.0 0.0 copy-start.1
  330.1 2.4 copy.34
  332.5 2.3 copy.35
  334.7 0.0 copy-done.1
  334.7 0.0 copy-start
  334.7 1.5 copy.36
  336.2 1.2 copy-done
  337.5 0.0 copy-start.2
  337.5 1.5 copy.37
  339.0 1.2 copy-done.2
  340.2 0.0 copy-start.6
  340.2 0.0 copy-start.5
  340.2 0.0 copy-start.4
  340.2 0.0 copy-start.3
  340.2 1.5 copy.38
  341.7 0.0 copy-done.6
  341.7 0.6 copy.39
  342.3 0.0 copy-done.5
  342.3 0.6 copy.40
  342.9 0.0 copy-done.4
  342.9 0.6 copy.41
  343.5 0.0 copy-done.3
  343.5 0.6 copy.42
  (3 shorter events, 0.1 us)
Async XLA Ops:
  330.0 4.7 %copy-start.1 = (f32[656,1024]{1,0:T(8,128)S(1)}, f32[656,1024]{1,0:T(8,128)}, u32[]{:S(2)}) copy-start(f32[656,1024]{1,0:T(8,128)} %get-tuple-element.51) | copy-start | bytes 8060932
  334.7 2.7 copy-start
  337.5 2.7 copy-start.2
  340.2 1.5 copy-start.6
  340.2 2.1 copy-start.5
  340.2 2.7 copy-start.4
  340.2 3.3 copy-start.3
where the time goes:
time: 352 us; the launch traced here: 345 us
  Pallas kernels  322 us (91%)
  local copies, waits for them, and re-layouts  18.9 us (5%)
    pallas_call x2, Pallas kernels, comm_call(): pl.pallas_call(kernel, out_shape=outs, in_specs=in_specs, out_specs=out_s...  196 us
    pallas_call x1, Pallas kernels, layer_both_ways(): pl.pallas_call(kernel, out_shape=outs, in_specs=[VMEM_SPEC] * len(ins), o...  127 us
    unnamed x24, local copies, waits for them, and re-layouts  14.9 us

commit v1 on v0

--- a/solution.py
+++ b/solution.py
@@ -938,10 +938,6 @@
         dkv_ref[...] = jnp.zeros_like(dkv_ref)
 
         def turn_back(i, carry):
-            @pl.when(i == 0)
-            def _():
-                line2.pair_up(6)
-                line2.pair_up(7)
             for part in range(2):
                 line2.receive(2 * i + part)
             moved, gain_part = norm_back(resid_ref[at(i)], gain_ref[1:2], sum2[at(i)].astype(f32))
@@ -968,6 +964,11 @@
             dq_ref[at(i)] = unstacked(nn_dot(ds_ref[...], kv_ref[:, 0:inner]))
             dkv_ref[:, 0:inner] = dkv_ref[:, 0:inner] + tn_dot(ds_ref[...], kq_ref[...])
             dkv_ref[:, inner:2 * inner] = dkv_ref[:, inner:2 * inner] + tn_dot(pl_ref[...], do_ref[...])
+
+            @pl.when(i == 0)
+            def _():
+                line2.pair_up(6)
+                line2.pair_up(7)
 
             @pl.when(i <= 1)
             def _():
@@ -1047,7 +1048,7 @@
     f32, low16 = jnp.float32, jnp.bfloat16
 
     def kernel(dp_ref, act_ref, at_ref, db_ref, dm_ref, mlp_ref, hid_ref, og_ref, mu_ref,
-               grad_ref, next_ref, x_ref, g_ref, norm_ref,
+               grad_ref, x_ref, g_ref, norm_ref,
                part, prx, rrx, mine, theirs, gprx, tot, other, early, mid, low, norm_own, *sems):
         place = Place()
         c = place.c
@@ -1081,7 +1082,6 @@
             sl = pl.ds(pl.multiple_of(i * 16, 16), 16)
             grad = grad_ref[sl]
             after = muon_beta * mu_ref[sl] + (1.0 - muon_beta) * grad
-            next_ref[sl] = after
             direction = (1.0 - muon_beta) * grad + muon_beta * after
             x_ref[sl] = direction.astype(low16)
             square = direction * direction
@@ -1168,7 +1168,7 @@
     rows_low = pltpu.VMEM((total_rows, width), low16)
     packed = pltpu.VMEM((5 * tile + 8, tile), f32)
     outs = (
-        jax.ShapeDtypeStruct((local_rows, width), f32), jax.ShapeDtypeStruct((local_rows, width), f32),
+        jax.ShapeDtypeStruct((local_rows, width), f32),
         jax.ShapeDtypeStruct((local_rows, width), low16), jax.ShapeDtypeStruct((width, width), f32),
         jax.ShapeDtypeStruct((8, 128), f32),
     )
@@ -1183,7 +1183,7 @@
     return high, (value - high.astype(jnp.float32)).astype(jnp.bfloat16)
 
 
-def iterate(gram, norm, direction_low, own_block, normed_term, branch_term, tokens_in, resid, dresid, dgain_rows, norm_gains, adam_first,
+def iterate(gram, norm, direction_low, normed_term, branch_term, tokens_in, resid, dresid, dgain_rows, norm_gains, adam_first,
             adam_second, ident):
     rows, width = direction_low.shape
     tile = 256
@@ -1199,9 +1199,9 @@
     cc = ns_third * ns_third
     correction = 1.0 - adam_beta**STEP
 
-    def kernel(g_ref, n_ref, d_ref, w_ref, t3_ref, b2_ref, tok_ref, r_ref, dres_ref, dgr_ref, gain_ref, af_ref, as_ref,
-               u_ref, lo_ref, tg_ref, gg_ref, afn_ref, asn_ref, gu_ref,
-               p_ref, ph, pl_, hh, hl, uh, ul, mx, x_ref, early, mid, low, total, held, dg_ref, *sems):
+    def kernel(g_ref, n_ref, d_ref, t3_ref, b2_ref, tok_ref, r_ref, dres_ref, dgr_ref, gain_ref, af_ref, as_ref,
+               x_ref, lo_ref, tg_ref, gg_ref, afn_ref, asn_ref, gu_ref,
+               p_ref, ph, pl_, hh, hl, uh, ul, mx, early, mid, low, total, held, dg_ref, *sems):
         place = Place()
         s1, r1, s2, r2, s3, r3, sg, rg = sems
         me = place.f * 2 + place.c
@@ -1350,15 +1350,25 @@
                 gains_copy(shift).start()
 
         def body(sweep, carry):
-            @pl.when(sweep >= 1)
+            middle = jnp.logical_and(sweep >= 1, sweep < ITERS - 1)
+
+            @pl.when(sweep == ITERS - 1)
             def _():
                 join_some(4 * sweep - 4)
             squares()
 
-            @pl.when(sweep >= 1)
+            @pl.when(middle)
+            def _():
+                join_some(4 * sweep - 4)
+
+            @pl.when(sweep == ITERS - 1)
             def _():
                 join_some(4 * sweep - 2)
             rotate_rows()
+
+            @pl.when(middle)
+            def _():
+                pair_some(4 * sweep)
 
             @pl.when(sweep < ITERS - 1)
             def _():
@@ -1369,7 +1379,13 @@
                     spread_out(bc * square + cc * cube, uh, ul, k)
                     p_ref[sl, cols] = aa * p_ref[sl, cols] + ab * square + bbac * cube
 
-                pair_some(4 * sweep)
+                @pl.when(sweep >= 1)
+                def _():
+                    join_some(4 * sweep - 2)
+
+                @pl.when(sweep == 0)
+                def _():
+                    pair_some(0)
                 for k in range(parts):
                     sl, cols = pl.ds(k * tile, tile), pl.ds(k * tile, width - k * tile)
                     value = p_ref[sl, cols] + product(hh, hl, uh, ul, k)
@@ -1382,10 +1398,6 @@
             return carry
 
         lax.fori_loop(0, ITERS, body, 0)
-        spread = jnp.where(place.f == 0, 0.2 * math.sqrt(3 * D), jnp.where(place.f == 1, 0.2 * math.sqrt(D), jnp.where(
-            place.f == 2, 0.2 * math.sqrt(2 * FF), 0.2 * math.sqrt(FF)))).astype(jnp.float32)
-        u_ref[...] = -muon_rate * (spread * x_ref[...] + decay_rate * w_ref[...].astype(jnp.float32))
-
         for shift in range(1, 8):
             gains_copy(shift).wait()
         grads = held[0]
@@ -1422,9 +1434,9 @@
     outs = (jax.ShapeDtypeStruct((rows, width), f32), narrow, narrow, small, small, small, small)
     full = pltpu.VMEM((width, width), low16)
     line = pltpu.VMEM((2 * tokens, width), low16)
-    scratch = [pltpu.VMEM((width, width), f32)] + [full] * 7 + [pltpu.VMEM((rows, width), f32)] + [line] * 4
+    scratch = [pltpu.VMEM((width, width), f32)] + [full] * 7 + [line] * 4
     scratch += [pltpu.VMEM((8, 8, width), f32), pltpu.VMEM((8, width), f32)] + [dma(chunks)] * 6 + [dma(8)] * 2
-    ins = (gram, norm, direction_low, own_block, normed_term, branch_term, tokens_in, resid, dresid, dgain_rows, norm_gains,
+    ins = (gram, norm, direction_low, normed_term, branch_term, tokens_in, resid, dresid, dgain_rows, norm_gains,
            adam_first, adam_second)
     return comm_call(kernel, outs, ins, [VMEM_SPEC] * len(ins), (VMEM_SPEC,) * len(outs), scratch, ident)
 
@@ -1452,15 +1464,21 @@
         jnp.tile(cosine, (1, heads_dev)), jnp.tile(sine_table, (1, heads_dev)),
         seg_query.reshape(token_count, 1), jnp.concatenate([seg_query, seg_other]).reshape(1, full_len), counts, 0,
     )
-    grad_block, muon_next, direction_low, gram, norm_total = tail_grams(
+    momentum = muon_state.reshape(local_rows, model_width)
+    grad_block, direction_low, gram, norm_total = tail_grams(
         (dprojected, act_in, attn_in, dbranch_one, dmixed, mlp_in, hidden, out_grad.reshape(token_count, model_width)),
-        muon_state.reshape(local_rows, model_width), counts, 1,
+        momentum, counts, 1,
     )
     direction_scale = jnp.log(jnp.sqrt(norm_total[0, 0])).reshape(1)
-    weight_update, layer_out, tokens_grad, gain_grads, adam_first_next, adam_second_next, gain_update = iterate(
-        gram, norm_total, direction_low, own_block, dnormed_one_term, branch_two_term,
+    ortho, layer_out, tokens_grad, gain_grads, adam_first_next, adam_second_next, gain_update = iterate(
+        gram, norm_total, direction_low, dnormed_one_term, branch_two_term,
         tokens.reshape(token_count, model_width), resid, dresid, dgain_rows, norm_gains, adam_first, adam_second, 2,
     )
+    muon_next = muon_beta * momentum + (1.0 - muon_beta) * grad_block
+    owner_index = lax.axis_index("fsdp")
+    spreads = [0.2 * math.sqrt(3 * D), 0.2 * math.sqrt(D), 0.2 * math.sqrt(2 * FF), 0.2 * math.sqrt(FF)]
+    spread = jnp.sum(jnp.where(jnp.arange(4) == owner_index, jnp.array(spreads, jnp.float32), 0.0))
+    weight_update = -muon_rate * (spread * ortho + decay_rate * own_block.astype(jnp.float32))
     layer_out = layer_out.reshape(tokens.shape)
     tokens_grad = tokens_grad.reshape(tokens.shape)
     block_shape = (1, 1, local_rows, model_width)

time: 352 us -> 344 us (0.977)
  Pallas kernels: 322 us -> 313 us
  other arithmetic: 1.61 us -> 10.3 us
  local copies, waits for them, and re-layouts: 18.9 us -> 11.3 us
    pallas_call x2, Pallas kernels: 196 us -> 186 us  [comm_call(): pl.pallas_call(kernel, out_shape=outs, in_specs=in_specs, out_specs=out_s...]
    unnamed x24 -> x26, local copies, waits for them, and re-layouts: 14.9 us -> 7.31 us
    reshape x0 -> x1, other arithmetic: none -> 7.43 us  [per_device_block(): weight_update.reshape(block_shape)]
where the time goes in v1:
time: 344 us; the launch traced here: 337 us
  Pallas kernels  313 us (91%)
  local copies, waits for them, and re-layouts  11.3 us (3%)
  other arithmetic  10.3 us (3%)
    pallas_call x2, Pallas kernels, comm_call(): pl.pallas_call(kernel, out_shape=outs, in_specs=in_specs, out_specs=out_s...  186 us
    pallas_call x1, Pallas kernels, layer_both_ways(): pl.pallas_call(kernel, out_shape=outs, in_specs=[VMEM_SPEC] * len(ins), o...  126 us
    reshape x1, other arithmetic, per_device_block(): weight_update.reshape(block_shape)  7.43 us
    unnamed x26, local copies, waits for them, and re-layouts  7.31 us

profile of v1, /device:TPU:0, one launch (start us, length us, event | category | flops | bytes accessed | tf_op | source)
XLA Modules:
  0.0 336.9 jit_solution(6010970163446441304)
XLA Ops:
  0.6 1.3 fusion.2
  1.9 0.7 convert_element_type.7
  2.6 0.7 constant_dynamic-slice_fusion
  3.3 0.6 pad_add_fusion
  3.9 0.1 broadcast_multiply_fusion
  4.0 0.2 fusion
  4.2 0.9 copy.24.sc_ref
  5.2 1.0 copy.23.sin_ref
  6.2 1.0 copy.22.cos_ref
  7.2 126.0 %shard_map.177 = (bf16[512,1024]{1,0:T(8,128)(2,1)}, bf16[512,256]{1,0:T(8,128)(2,1)}, f32[512,1024]{1,0:T(8,128)}, bf16[512,1024]{1,0:T(8,128)(2,1)}, bf16[512,...) custom-call(bf16[512,1024]{1,0:T(8,128)(2,1)} %bitcast.25, ...), custom_call_target="tpu_custom_call" | custom-call | tf_op jit(solution)/shard_map/pallas_call | solution.py:1026
  133.3 94.8 %shard_map.178 = (f32[656,1024]{1,0:T(8,128)}, bf16[656,1024]{1,0:T(8,128)(2,1)}, f32[1024,1024]{1,0:T(8,128)}, f32[8,128]{1,0:T(8,128)}) custom-call(bf16[512,768]{1,0:T(8,128)(2,1)} %get-tuple-element.33.dp_ref, bf16[512,1024]{1,0:T(8,128)(2,1)} %get-tuple-element.34.act_ref, bf16[512,256]{1,0:T(8,128)(2,1)} %get-tuple-element.35.at_ref, ...), custom_call_target="tpu_custom_call" | custom-call | tf_op jit(solution)/shard_map/pallas_call | solution.py:637
  228.1 1.2 slice.3
  230.0 0.0 copy-start
  230.0 0.0 copy-start.2
  230.0 91.7 %shard_map.179 = (f32[656,1024]{1,0:T(8,128)}, bf16[512,1024]{1,0:T(8,128)(2,1)}, bf16[512,1024]{1,0:T(8,128)(2,1)}, f32[2,1024]{1,0:T(2,128)}, f32[2,1024]{1,0:...) custom-call(f32[1024,1024]{1,0:T(8,128)} %get-tuple-element.40.g_ref, f32[8,128]{1,0:T(8,128)} %get-tuple-element.41.n_ref, ...), custom_call_target="tpu_custom_call" | custom-call | tf_op jit(solution)/shard_map/pallas_call | solution.py:637
  321.7 0.0 copy-done
  321.7 0.0 copy-done.2
  321.7 0.0 copy-start.4
  321.7 0.0 copy-start.3
  321.7 7.4 %multiply_bitcast_fusion = (f32[1,1,656,1024]{3,2,1,0:T(8,128)}, f32[1,1,656,1024]{3,2,1,0:T(8,128)}) fusion(f32[656,1024]{1,0:T(8,128)} %get-tuple-element.51, f32[]{:T(128)} %fusion.2, bf16[1,1,656,1024]{3,2,1,0:T(8,128)(2,1)S(1)} %copy-done.2, f32[656,1024]{1,0:T(8,128)} %get-tuple-element.50, f32[1,1,656,1024]{3,2,1,0:T(8,128)S(1)} %copy-done), kind=kLoop, calls=%fused_computation | loop fusion | flops 4702208 | bytes 14778372 | tf_op jit(solution)/shard_map/reshape | solution.py:1490
  329.1 0.0 copy-start.1
  329.1 0.0 copy-done.4
  329.1 1.0 copy.33
  330.1 0.0 copy-done.3
  330.1 1.0 copy.34
  331.1 0.6 copy-done.1
  331.7 0.0 copy-start.8
  331.7 0.0 copy-start.7
  331.7 0.0 copy-start.6
  331.7 0.0 copy-start.5
  331.7 1.5 copy.35
  333.2 0.0 copy-done.8
  333.2 0.6 copy.36
  333.8 0.0 copy-done.7
  333.8 0.6 copy.37
  334.4 0.0 copy-done.6
  334.4 0.6 copy.38
  335.0 0.0 copy-done.5
  335.0 0.6 copy.39
  (3 shorter events, 0.1 us)
Async XLA Ops:
  230.0 91.7 %copy-start = (f32[1,1,656,1024]{3,2,1,0:T(8,128)S(1)}, f32[1,1,656,1024]{3,2,1,0:T(8,128)}, u32[]{:S(2)}) copy-start(f32[1,1,656,1024]{3,2,1,0:T(8,128)} %param.13) | copy-start | bytes 8060932
  230.0 91.7 %copy-start.2 = (bf16[1,1,656,1024]{3,2,1,0:T(8,128)(2,1)S(1)}, bf16[1,1,656,1024]{3,2,1,0:T(8,128)(2,1)}, u32[]{:S(2)}) copy-start(bf16[1,1,656,1024]{3,2,1,0:T(8,128)(2,1)} %param.12) | copy-start | bytes 4030468
  321.7 7.5 %copy-start.4 = (bf16[512,1024]{1,0:T(8,128)(2,1)S(1)}, bf16[512,1024]{1,0:T(8,128)(2,1)}, u32[]{:S(2)}) copy-start(bf16[512,1024]{1,0:T(8,128)(2,1)} %get-tuple-element.48) | copy-start | bytes 3145732
  321.7 8.4 %copy-start.3 = (bf16[512,1024]{1,0:T(8,128)(2,1)S(1)}, bf16[512,1024]{1,0:T(8,128)(2,1)}, u32[]{:S(2)}) copy-start(bf16[512,1024]{1,0:T(8,128)(2,1)} %get-tuple-element.49) | copy-start | bytes 3145732
  329.1 2.5 copy-start.1
  331.7 1.5 copy-start.8
  331.7 2.1 copy-start.7
  331.7 2.7 copy-start.6
  331.7 3.3 copy-start.5
